TPU v7x, 32 devices: a whole 2x2x4 slice. The times are simulated.
32 devices in a mesh: section: 2 (over x), dp: 16 (over z, y, core).
Axes of the slice: x: 2, y: 2, z: 4, core: 2. Of those that a mesh axis runs over, the one named last changes fastest.
Arguments:
- activations: bfloat16 [4, 256, 4608], P('section', 'dp'), may hold values from -6 to 6
- section_sources: int32 [4], replicated, may hold values from 0 to 3, as said below
- accumulators: float32 [256, 4, 4608], P('dp', 'section'), may hold values from -6 to 6
- block_sources: int32 [256], replicated, may hold values from 0 to 255, as said below
- loss_terms: float32 [2, 16], P('section', 'dp'), may hold values from 0.35 to 6
- pre_gain: float32 [2, 4608], P('section'), may hold values from 0.1 to 1.9
- query_weight: bfloat16 [2, 4608, 2048], P('section', None, 'dp'), may hold values from -0.09375 to 0.09375
- keyval_weight: bfloat16 [2, 4608, 2048], P('section', None, 'dp'), may hold values from -0.09375 to 0.09375
- output_weight: bfloat16 [2, 2048, 4608], P('section', 'dp'), may hold values from -0.125 to 0.125
- post_gain: float32 [2, 4608], P('section'), may hold values from 0.1 to 1.9
Outputs:
- new_activations: bfloat16 [4, 256, 4608], P('section', 'dp')
- new_accumulators: float32 [256, 4, 4608], P('dp', 'section')
- check_out: bfloat16 [2, 256, 4608], P('section', 'dp')
Inputs may be any that keep to these rules, and one draw needn't show every extreme that they name: `section_sources`: A permutation; each old section's micro-batches fill 1 slots of each new section. `block_sources`: A permutation; each old data index's blocks fill 1 block of each new data index.
All inputs are finite; a program needn't handle non-finite values.
Results may differ from a plain program's by a relative error of at most 0.014.
Values may be sent and summed in bfloat16 or wider, within the bound.
A program may use at most 64 MiB of HBM per device.

v0:
```python
import functools

import jax
import jax.numpy as jnp
import numpy as np
from jax import lax
from jax.experimental import pallas as pl
from jax.experimental.pallas import tpu as pltpu
from jax.sharding import PartitionSpec as P

LANES = 128
VMEM_BYTES = 67043328
CHUNKS = 6
F32 = jnp.float32
BF16 = jnp.bfloat16


def pick(table, own, groups, per_group, peer, rank):
    def visit(j, carry):
        seen, found = carry
        source = table[peer * per_group + j]
        mine = (source // per_group == own).astype(jnp.int32)
        hit = mine * (seen == rank).astype(jnp.int32)
        return seen + mine, found + hit * (source % per_group)

    zero = jnp.int32(0)
    return lax.fori_loop(0, per_group, visit, (zero, zero), unroll=True)[1]


def origin(table, own, per_group, per_peer, entry):
    owner = table[own * per_group + entry] // per_group
    if per_peer == 1:
        return owner, 0

    def visit(j, seen):
        same = table[own * per_group + j] // per_group == owner
        return seen + same.astype(jnp.int32) * (j < entry).astype(jnp.int32)

    return owner, lax.fori_loop(0, per_group, visit, jnp.int32(0))


def rotary_tables(length, width):
    half = width // 2
    freqs = np.float32(10000.0) ** (np.float32(-2.0) * np.arange(half, dtype=np.float32) / np.float32(width))
    angles = np.arange(length, dtype=np.float32)[:, None] * freqs.astype(np.float32)[None, :]
    cosine, sine = np.cos(angles.astype(np.float64)), np.sin(angles.astype(np.float64))
    return np.stack(
        [np.concatenate([cosine, cosine], 1), np.concatenate([-sine, sine], 1)]
    ).astype(np.float32)


def kernel(
    dims,
    secs_hbm, blks_hbm, loss_hbm, act_hbm, acc_hbm, pre_hbm, wq_hbm, wkv_hbm, wo_hbm, post_hbm, rot_hbm,
    moved, accout, outbuf,
    secs, blks, loss, act, acc, pre, post, rot, w, wo,
    stage, actrecv, sacc, racc,
    gath, qkv, att, att_in, part, ring_in, ring_out,
    load_sem, act_out, act_sem, w_sem, wo_sem, blk_sem, ag_out, ag_sem, fwd_sem, att_sem, ring_done, ring_sem,
):
    n_sec, n_dp = dims
    mb, toks, d = act.shape
    blk, brows, _ = acc.shape
    act_pp, blk_pp = mb // n_sec, blk // n_dp
    chips = n_dp // 2
    far = chips // 2
    kd = d // CHUNKS
    length = n_dp * toks
    hd = wq_hbm.shape[2]
    sec, me = lax.axis_index("section"), lax.axis_index("dp")
    core, chip = me % 2, me // 2
    side, rung = chip % 2, chip // 2
    pos = rung * (1 - side) + (chips - 1 - rung) * side

    def chip_at(p):
        q = (p + 2 * chips) % chips
        s = q // (chips // 2)
        return 2 * (q * (1 - s) + (chips - 1 - q) * s) + s

    def device(p):
        return {"dp": 2 * chip_at(p) + core}

    partner = {"dp": me + 1 - 2 * core}

    def remote(src, dst, send_sem, recv_sem, dev):
        return pltpu.make_async_remote_copy(
            src_ref=src, dst_ref=dst, send_sem=send_sem, recv_sem=recv_sem,
            device_id=dev, device_id_type=pl.DeviceIdType.MESH,
        )

    barrier = pltpu.get_barrier_semaphore()
    for o in range(1, n_sec):
        pl.semaphore_signal(barrier, inc=1, device_id={"section": (sec + o) % n_sec},
                            device_id_type=pl.DeviceIdType.MESH)
    for near in (device(pos + 1), device(pos - 1), partner):
        pl.semaphore_signal(barrier, inc=1, device_id=near, device_id_type=pl.DeviceIdType.MESH)

    kv_cols = pl.ds(pl.multiple_of(hd + core * hd, LANES), hd)
    q_cols = pl.ds(0, hd)
    wo_rows = pl.ds(pl.multiple_of(core * hd, LANES), hd)
    names = ("secs", "act", "pre", "wkv", "wo", "blks", "loss", "acc", "wq", "rot", "post")
    pairs = [
        (secs_hbm, secs), (act_hbm, act), (pre_hbm, pre), (wkv_hbm.at[0], w.at[:, kv_cols]),
        (wo_hbm.at[0], wo.at[wo_rows]), (blks_hbm, blks), (loss_hbm, loss), (acc_hbm, acc),
        (wq_hbm.at[0], w.at[:, q_cols]), (rot_hbm, rot), (post_hbm, post),
    ]
    loads = {
        name: pltpu.make_async_copy(src, dst, load_sem.at[i])
        for i, (name, (src, dst)) in enumerate(zip(names, pairs))
    }
    for name in names:
        loads[name].start()

    loads["secs"].wait()
    loads["act"].wait()
    for q in range(n_sec):
        for r in range(act_pp):
            block = act[pick(secs, sec, n_sec, mb, q, r)]
            for k in range(CHUNKS):
                stage[q, k, r] = block[:, k * kd:(k + 1) * kd]
    pl.semaphore_wait(barrier, n_sec - 1 + 3)
    act_copies = [[] for _ in range(CHUNKS)]
    for k in range(CHUNKS):
        for o in range(1, n_sec):
            q = (sec + o) % n_sec
            copy = remote(stage.at[q, k], actrecv[k].at[sec], act_out.at[o - 1], act_sem.at[o - 1, k], {"section": q})
            copy.start()
            act_copies[k].append(copy)
    for k in range(CHUNKS):
        actrecv[k][sec] = stage[sec, k]

    loads["wkv"].wait()
    kv_copy = remote(w.at[:, kv_cols], w.at[:, kv_cols], w_sem.at[0], w_sem.at[1], partner)
    kv_copy.start()
    loads["wo"].wait()
    wo_copy = remote(wo.at[wo_rows], wo.at[wo_rows], wo_sem.at[0], wo_sem.at[1], partner)
    wo_copy.start()
    loads["pre"].wait()

    for name in ("acc", "blks", "loss"):
        loads[name].wait()
    term = jnp.full((brows, LANES), loss[0, 0], F32)
    high = term.astype(BF16).astype(F32)
    lane = lax.broadcasted_iota(jnp.int32, (brows, LANES), 1)
    row = lax.broadcasted_iota(jnp.int32, (brows, LANES), 0)
    tail = jnp.where(row > 0, 0.0, jnp.where(lane == 0, high, jnp.where(lane == 1, term - high, 0.0)))

    def pack(p, carry):
        for r in range(blk_pp):
            sacc[p, r, :, pl.ds(0, d)] = acc[pick(blks, me, n_dp, blk, p, r)].astype(BF16)
            sacc[p, r, :, pl.ds(d, LANES)] = tail.astype(BF16)
        return carry

    lax.fori_loop(0, n_dp, pack, 0)
    racc[me] = sacc[me]

    def hops(way, k):
        return far if (k < CHUNKS // 2) == (way == 0) else far - 1

    step_of = (1, -1)

    def width(k):
        return kd + LANES if k == CHUNKS - 1 else kd

    def blocks_of(k, c, places):
        return gath.at[k, c, places, :, pl.ds(0, width(k))]

    def gather_copy(way, hop, k, place):
        block = blocks_of(k, core, place)
        return remote(block, block, ag_out.at[k], ag_sem.at[way, hop - 1, k], device(pos + step_of[way]))

    def pass_on(place, k):
        block = blocks_of(k, core, place)
        remote(block, block, fwd_sem.at[0, k], fwd_sem.at[1, k], partner).start()

    square = jnp.zeros((toks, 1), F32)
    for k in range(CHUNKS):
        for copy in act_copies[k]:
            copy.wait_recv()
        owner, number = origin(secs, sec, mb, act_pp, 0)
        piece = actrecv[k][owner, number].astype(F32)
        square = square + jnp.sum(piece * piece, axis=-1, keepdims=True)
        gath[k, core, chip, :, pl.ds(0, kd)] = (piece * pre[:, k * kd:(k + 1) * kd]).astype(BF16)
        if k == CHUNKS - 1:
            root = jnp.broadcast_to(lax.rsqrt(square / d + 1e-06), (toks, LANES))
            high = root.astype(BF16).astype(F32)
            lane = lax.broadcasted_iota(jnp.int32, (toks, LANES), 1)
            gath[k, core, chip, :, pl.ds(kd, LANES)] = jnp.where(
                lane == 0, high, jnp.where(lane == 1, root - high, 0.0)).astype(BF16)
        for way in range(2):
            gather_copy(way, 1, k, chip).start()
        pass_on(chip, k)

    other = me + 1 - 2 * core

    def project(k):
        block = blocks_of(k, 1 - core, slice(None))
        remote(block, block, fwd_sem.at[0, k], fwd_sem.at[1, k], partner).wait_recv()
        rows = gath[k, :, :, :, pl.ds(0, kd)].reshape(length, kd)
        terms = jnp.dot(rows, w[k * kd:(k + 1) * kd, :], preferred_element_type=F32)
        qkv[...] = terms if k == 0 else qkv[...] + terms

    def send_block(peer):
        remote(sacc.at[peer], racc.at[me], blk_sem.at[0], blk_sem.at[1], {"dp": peer}).start()

    def send_blocks(places):
        for way, hop in places:
            for c in range(2):
                send_block(2 * chip_at(pos + step_of[way] * hop) + (core + c) % 2)

    send_block(other)
    for hop in range(1, far + 1):
        for k in range(CHUNKS):
            for way in range(2):
                if hop > hops(way, k):
                    continue
                place = chip_at(pos - step_of[way] * hop)
                gather_copy(way, hop, k, place).wait_recv()
                if hop < hops(way, k):
                    gather_copy(way, hop + 1, k, place).start()
                pass_on(place, k)
            if hop == far and k == 0:
                kv_copy.wait_recv()
                loads["wq"].wait()
            elif hop == far:
                project(k - 1)
        if hop == far - 1:
            send_blocks([(way, h) for h in range(1, far) for way in range(2)])
    send_blocks([(0, far)])
    project(CHUNKS - 1)

    loads["rot"].wait()
    parts = gath[CHUNKS - 1, :, :, :, pl.ds(kd, LANES)].reshape(length, LANES).astype(F32)
    root = jnp.sum(parts, axis=-1, keepdims=True)
    cosine, sine = rot[0] * root, rot[1] * root

    def turned(v):
        return (v * cosine + pltpu.roll(v, hd // 2, 1) * sine).astype(BF16)

    def token_at(shape, dim):
        row = lax.broadcasted_iota(jnp.int32, shape, dim)
        block = row // toks
        return (block % chips * 2 + block // chips) * toks + row % toks

    queries = turned(qkv[:, 0:hd])
    keys = turned(qkv[:, hd:2 * hd])
    values = (qkv[:, 2 * hd:3 * hd] * root).astype(BF16)
    scores = lax.dot_general(queries, keys, (((1,), (1,)), ((), ())), preferred_element_type=F32)
    scores = scores * ((d / n_dp) ** (-0.5) / 50.0)
    expd = jnp.where(token_at((1, length), 1) <= token_at((length, 1), 0), jnp.exp(50.0 * jnp.tanh(scores)), 0.0)
    denominator = jnp.sum(expd, axis=-1, keepdims=True)
    numer = jnp.dot(expd.astype(BF16), values, preferred_element_type=F32)
    attended = (numer / denominator).astype(BF16)

    att[...] = attended.reshape(2, chips, toks, hd)
    att_copy = remote(att.at[1 - core], att_in, att_sem.at[0], att_sem.at[1], partner)
    att_copy.start()
    wo_copy.wait_recv()
    ours = att[core].reshape(chips * toks, hd)
    att_copy.wait_recv()
    theirs = att_in[...].reshape(chips * toks, hd)
    even = core == 0
    both = jnp.concatenate([jnp.where(even, ours, theirs), jnp.where(even, theirs, ours)], axis=1)

    def ring_copy(way, step, k):
        return remote(ring_out.at[k, way * far + step - 1], ring_in.at[k, way * far + step - 1],
                      ring_done.at[k], ring_sem.at[way, step - 1, k], device(pos + step_of[way]))

    for k in range(CHUNKS):
        terms = jnp.dot(both, wo[:, k * kd:(k + 1) * kd], preferred_element_type=F32)
        part[k] = terms.reshape(chips, toks, kd)
        for way in range(2):
            ring_out[k, way * far] = part[k, chip_at(pos + step_of[way] * hops(way, k))].astype(BF16)
            ring_copy(way, 1, k).start()
    for j in range(mb):
        owner, number = origin(secs, sec, mb, act_pp, j)
        for k in range(CHUNKS):
            moved[j, :, k * kd:(k + 1) * kd] = actrecv[k][owner, number]

    others = pl.ds(0, n_dp - 1)
    all_blocks = remote(sacc.at[others], racc.at[others], blk_sem.at[0], blk_sem.at[1], partner)
    all_blocks.wait_recv()
    scale_sum = jnp.sum(racc[:, 0, :, pl.ds(d, LANES)].astype(F32), axis=0)
    factor = n_dp / jnp.sum(jnp.sum(scale_sum, axis=0, keepdims=True), axis=1, keepdims=True)

    def unpack(b, carry):
        owner, number = origin(blks, me, blk, blk_pp, b)
        accout[b] = racc[owner, number, :, pl.ds(0, d)].astype(F32) * factor
        return carry

    lax.fori_loop(0, blk, unpack, 0)

    for step in range(1, far):
        for k in range(CHUNKS):
            for way in range(2):
                left = hops(way, k) - step
                if left < 1:
                    continue
                ring_copy(way, step, k).wait_recv()
                total = part[k, chip_at(pos + step_of[way] * left)] + ring_in[k, way * far + step - 1].astype(F32)
                ring_out[k, way * far + step] = total.astype(BF16)
                ring_copy(way, step + 1, k).start()

    pieces = []
    for k in range(CHUNKS):
        total = part[k, chip_at(pos)]
        for way in range(2):
            step = hops(way, k)
            ring_copy(way, step, k).wait_recv()
            total = total + ring_in[k, way * far + step - 1].astype(F32)
        pieces.append(total)
    loads["post"].wait()
    square = sum(jnp.sum(t * t, axis=-1, keepdims=True) for t in pieces)
    scale = lax.rsqrt(square / d + 1e-06)
    for k in range(CHUNKS):
        cols = slice(k * kd, (k + 1) * kd)
        outbuf[0, :, cols] = (
            moved[0, :, cols].astype(F32) + pieces[k] * scale * post[:, cols]
        ).astype(BF16)
    for copy in (kv_copy, wo_copy, att_copy, all_blocks):
        copy.wait_send()
    for o in range(1, n_sec):
        q = (sec + o) % n_sec
        remote(stage.at[q], stage.at[q], act_out.at[o - 1], act_sem.at[o - 1, 0], {"section": q}).wait_send()
    for k in range(CHUNKS):
        for places, sem in ((slice(None), fwd_sem.at[0, k]), (pl.ds(0, chips - 1), ag_out.at[k])):
            block = blocks_of(k, core, places)
            remote(block, block, sem, fwd_sem.at[1, k], partner).wait_send()
        block = ring_out.at[k, pl.ds(0, chips - 1)]
        remote(block, block, ring_done.at[k], fwd_sem.at[1, k], partner).wait_send()


def write_out(moved, accout, outbuf, moved_hbm, newacc_hbm, check_hbm, sems):
    copies = [
        pltpu.make_async_copy(src, dst, sems.at[i])
        for i, (src, dst) in enumerate([(accout, newacc_hbm), (moved, moved_hbm), (outbuf, check_hbm)])
    ]
    for copy in copies:
        copy.start()
    for copy in copies:
        copy.wait()


def make_on_device(n_sec, n_dp):
    def on_device(activations, section_sources, accumulators, block_sources, loss_terms,
                  pre_gain, query_weight, keyval_weight, output_weight, post_gain):
        mb, toks, d = activations.shape
        blk, brows, _ = accumulators.shape
        hd = query_weight.shape[2]
        chips, far, kd, length = n_dp // 2, n_dp // 4, d // CHUNKS, n_dp * toks
        order = np.arange(length).reshape(chips, 2, toks).transpose(1, 0, 2).reshape(-1)
        rot = jnp.asarray(rotary_tables(length, hd)[:, order])
        smem = pltpu.SMEM
        in_hbm = pl.BlockSpec(memory_space=pltpu.HBM)
        vmem = pl.BlockSpec(memory_space=pltpu.VMEM)
        dma = pltpu.SemaphoreType.DMA
        act_pp, blk_pp = mb // n_sec, blk // n_dp
        out_bytes = activations.size * 2 + accumulators.size * 4 + toks * d * 2
        held = pl.pallas_call(
            functools.partial(kernel, (n_sec, n_dp)),
            out_shape=(
                pltpu.VMEM(activations.shape, BF16),
                pltpu.VMEM(accumulators.shape, F32),
                pltpu.VMEM((1, toks, d), BF16),
            ),
            in_specs=[in_hbm] * 11,
            out_specs=(vmem,) * 3,
            scratch_shapes=[
                smem(section_sources.shape, jnp.int32),
                smem(block_sources.shape, jnp.int32),
                smem((1, 1), F32),
                pltpu.VMEM(activations.shape, BF16),
                pltpu.VMEM(accumulators.shape, F32),
                pltpu.VMEM((1, d), F32),
                pltpu.VMEM((1, d), F32),
                pltpu.VMEM(rot.shape, F32),
                pltpu.VMEM((d, 3 * hd), BF16),
                pltpu.VMEM((2 * hd, d), BF16),
                pltpu.VMEM((n_sec, CHUNKS, act_pp, toks, kd), BF16),
                (pltpu.VMEM((n_sec, act_pp, toks, kd), BF16),) * CHUNKS,
                pltpu.VMEM((n_dp, blk_pp, brows, d + LANES), BF16),
                pltpu.VMEM((n_dp, blk_pp, brows, d + LANES), BF16),
                pltpu.VMEM((CHUNKS, 2, chips, toks, kd + LANES), BF16),
                pltpu.VMEM((length, 3 * hd), F32),
                pltpu.VMEM((2, chips, toks, hd), BF16),
                pltpu.VMEM((chips, toks, hd), BF16),
                pltpu.VMEM((CHUNKS, chips, toks, kd), F32),
                pltpu.VMEM((CHUNKS, 2 * far, toks, kd), BF16),
                pltpu.VMEM((CHUNKS, 2 * far, toks, kd), BF16),
                dma((11,)),
                dma((n_sec - 1,)),
                dma((n_sec - 1, CHUNKS)),
                dma((2,)),
                dma((2,)),
                dma((2,)),
                dma((CHUNKS,)),
                dma((2, far, CHUNKS)),
                dma((2, CHUNKS)),
                dma((2,)),
                dma((CHUNKS,)),
                dma((2, far, CHUNKS)),
            ],
            compiler_params=pltpu.CompilerParams(
                collective_id=0, has_side_effects=True, vmem_limit_bytes=VMEM_BYTES - 2**16 - out_bytes
            ),
        )(section_sources, block_sources, loss_terms, activations, accumulators,
          pre_gain, query_weight, keyval_weight, output_weight, post_gain, rot)
        return pl.pallas_call(
            write_out,
            out_shape=(
                jax.ShapeDtypeStruct(activations.shape, BF16),
                jax.ShapeDtypeStruct(accumulators.shape, F32),
                jax.ShapeDtypeStruct((1, toks, d), BF16),
            ),
            in_specs=[vmem] * 3,
            out_specs=(in_hbm,) * 3,
            scratch_shapes=[dma((3,))],
            compiler_params=pltpu.CompilerParams(vmem_limit_bytes=4 * 2**20),
        )(*held)

    return on_device


def solution(mesh):
    placed = (
        P("section", "dp", None),
        P(),
        P("dp", "section", None),
        P(),
        P("section", "dp"),
        P("section", None),
        P("section", None, "dp"),
        P("section", None, "dp"),
        P("section", "dp", None),
        P("section", None),
    )
    return jax.shard_map(
        make_on_device(mesh.shape["section"], mesh.shape["dp"]),
        mesh=mesh,
        in_specs=placed,
        out_specs=(P("section", "dp", None), P("dp", "section", None), P("section", "dp", None)),
        check_vma=False,
    )
```

profile of v0, /device:TPU:0, one launch (start us, length us, event | category | flops | bytes accessed | tf_op | source)
XLA Modules:
  0.0 45.2 jit_solution(10466330747779057398)
XLA Ops:
  1.3 42.9 %shard_map.130 = (bf16[2,16,4608]{2,1,0:T(8,128)(2,1)S(1)}, f32[16,2,4608]{2,1,0:T(2,128)S(1)}, bf16[1,16,4608]{2,1,0:T(8,128)(2,1)S(1)}) custom-call(s32[4]{0:T(128)} %secs_hbm.1, s32[256]{0:T(256)} %blks_hbm.1, f32[1,1]{1,0:T(1,128)S(6)} %copy.14.loss_hbm, bf16[2,16,4608]{2,1,0:T(8,128)(2,1)} %act_hbm.1, f32[16,2,4608]{2,1,0:T(2,128)} %acc_hbm.1, ...), custom_call_target="tpu_custom_call" | custom-call | tf_op jit(solution)/shard_map/pallas_call | solution.py:359
  44.2 1.0 %shard_map.131 = (bf16[2,16,4608]{2,1,0:T(8,128)(2,1)}, f32[16,2,4608]{2,1,0:T(2,128)}, bf16[1,16,4608]{2,1,0:T(8,128)(2,1)}) custom-call(bf16[2,16,4608]{2,1,0:T(8,128)(2,1)S(1)} %get-tuple-element.6.moved, f32[16,2,4608]{2,1,0:T(2,128)S(1)} %get-tuple-element.7.accout, bf16[1,16,4608]{2,1,0:T(8,128)(2,1)S(1)} %get-tuple-element.8.outbuf), custom_call_target="tpu_custom_call" | custom-call | tf_op jit(solution)/shard_map/pallas_call | solution.py:408
where the time goes:
time: 45.4 us; the launch traced here: 45.2 us
  Pallas kernels  43.9 us (97%)
  between operations  1.29 us (3%)
    pallas_call x1, Pallas kernels, on_device(): pl.pallas_call(functools.partial(kernel, (n_sec, n_dp)), out_shape=(pltpu...  42.9 us
    pallas_call x1, Pallas kernels, on_device(): pl.pallas_call(write_out, out_shape=(jax.ShapeDtypeStruct(activations.sha...  0.98 us

commit v1 on v0

--- a/solution.py
+++ b/solution.py
@@ -11,6 +11,9 @@
 LANES = 128
 VMEM_BYTES = 67043328
 CHUNKS = 6
+MIXED = (0, 3, 1, 4, 2, 5)
+AHEAD = ((0, 1, 3, 2, 4, 5), (3, 0, 4, 1, 5, 2))
+SORTED = ((0, 1, 2, 3, 4, 5), (3, 4, 5, 0, 1, 2))
 F32 = jnp.float32
 BF16 = jnp.bfloat16
 
@@ -53,10 +56,10 @@
     dims,
     secs_hbm, blks_hbm, loss_hbm, act_hbm, acc_hbm, pre_hbm, wq_hbm, wkv_hbm, wo_hbm, post_hbm, rot_hbm,
     moved, accout, outbuf,
-    secs, blks, loss, act, acc, pre, post, rot, w, wo,
+    secs, blks, loss, act, acc, pre, post, rot, turn, w, wo,
     stage, actrecv, sacc, racc,
-    gath, qkv, att, att_in, part, ring_in, ring_out,
-    load_sem, act_out, act_sem, w_sem, wo_sem, blk_sem, ag_out, ag_sem, fwd_sem, att_sem, ring_done, ring_sem,
+    gath, qs, kvs, part, ring_in, ring_out,
+    load_sem, act_out, act_sem, w_sem, wq_sem, wo_sem, blk_sem, ag_out, ag_sem, fwd_sem, ring_done, ring_sem,
 ):
     n_sec, n_dp = dims
     mb, toks, d = act.shape
@@ -95,8 +98,8 @@
     for near in (device(pos + 1), device(pos - 1), partner):
         pl.semaphore_signal(barrier, inc=1, device_id=near, device_id_type=pl.DeviceIdType.MESH)
 
-    kv_cols = pl.ds(pl.multiple_of(hd + core * hd, LANES), hd)
-    q_cols = pl.ds(0, hd)
+    kv_cols = pl.ds(pl.multiple_of(2 * hd + core * hd, LANES), hd)
+    q_cols = pl.ds(pl.multiple_of(core * hd, LANES), hd)
     wo_rows = pl.ds(pl.multiple_of(core * hd, LANES), hd)
     names = ("secs", "act", "pre", "wkv", "wo", "blks", "loss", "acc", "wq", "rot", "post")
     pairs = [
@@ -120,7 +123,7 @@
                 stage[q, k, r] = block[:, k * kd:(k + 1) * kd]
     pl.semaphore_wait(barrier, n_sec - 1 + 3)
     act_copies = [[] for _ in range(CHUNKS)]
-    for k in range(CHUNKS):
+    for k in MIXED:
         for o in range(1, n_sec):
             q = (sec + o) % n_sec
             copy = remote(stage.at[q, k], actrecv[k].at[sec], act_out.at[o - 1], act_sem.at[o - 1, k], {"section": q})
@@ -130,12 +133,17 @@
         actrecv[k][sec] = stage[sec, k]
 
     loads["wkv"].wait()
-    kv_copy = remote(w.at[:, kv_cols], w.at[:, kv_cols], w_sem.at[0], w_sem.at[1], partner)
-    kv_copy.start()
     loads["wo"].wait()
-    wo_copy = remote(wo.at[wo_rows], wo.at[wo_rows], wo_sem.at[0], wo_sem.at[1], partner)
-    wo_copy.start()
-    loads["pre"].wait()
+    loads["wq"].wait()
+
+    def whole(ref, sems):
+        return remote(ref, ref, sems.at[0], sems.at[1], partner)
+
+    kv_copy, q_copy = whole(w.at[:, kv_cols], w_sem), whole(w.at[:, q_cols], wq_sem)
+    wo_copy = whole(wo.at[wo_rows], wo_sem)
+
+    def share(ref, sems):
+        remote(ref, ref, sems.at[0], sems.at[1], partner).start()
 
     for name in ("acc", "blks", "loss"):
         loads[name].wait()
@@ -151,8 +159,8 @@
             sacc[p, r, :, pl.ds(d, LANES)] = tail.astype(BF16)
         return carry
 
-    lax.fori_loop(0, n_dp, pack, 0)
-    racc[me] = sacc[me]
+    lax.fori_loop(0, n_dp // 2, pack, 0)
+    loads["pre"].wait()
 
     def hops(way, k):
         return far if (k < CHUNKS // 2) == (way == 0) else far - 1
@@ -160,45 +168,59 @@
     step_of = (1, -1)
 
     def width(k):
-        return kd + LANES if k == CHUNKS - 1 else kd
-
-    def blocks_of(k, c, places):
-        return gath.at[k, c, places, :, pl.ds(0, width(k))]
-
-    def gather_copy(way, hop, k, place):
-        block = blocks_of(k, core, place)
-        return remote(block, block, ag_out.at[k], ag_sem.at[way, hop - 1, k], device(pos + step_of[way]))
-
-    def pass_on(place, k):
-        block = blocks_of(k, core, place)
-        remote(block, block, fwd_sem.at[0, k], fwd_sem.at[1, k], partner).start()
+        return kd + LANES if k == MIXED[-1] else kd
+
+    def slot(way, hop):
+        return 0 if hop == 0 else min(2 * hop - 1 + way, chips - 1)
+
+    def blocks_of(k, c, slots):
+        return gath.at[k, c, slots, :, pl.ds(0, width(k))]
+
+    def gather_copy(way, hop, k):
+        return remote(blocks_of(k, core, slot(way, hop - 1)), blocks_of(k, core, slot(way, hop)),
+                      ag_out.at[k], ag_sem.at[way, hop - 1, k], device(pos + step_of[way]))
+
+    near = 2 * (far - 2) + 1
+    spans = (slice(0, near), slice(near, chips))
+
+    def pass_on(j, k):
+        block = blocks_of(k, core, j)
+        remote(block, block, fwd_sem.at[0, k], fwd_sem.at[1 if j < near else 2, k], partner).start()
 
     square = jnp.zeros((toks, 1), F32)
-    for k in range(CHUNKS):
+    for k in MIXED:
         for copy in act_copies[k]:
             copy.wait_recv()
         owner, number = origin(secs, sec, mb, act_pp, 0)
         piece = actrecv[k][owner, number].astype(F32)
         square = square + jnp.sum(piece * piece, axis=-1, keepdims=True)
-        gath[k, core, chip, :, pl.ds(0, kd)] = (piece * pre[:, k * kd:(k + 1) * kd]).astype(BF16)
-        if k == CHUNKS - 1:
+        gath[k, core, 0, :, pl.ds(0, kd)] = (piece * pre[:, k * kd:(k + 1) * kd]).astype(BF16)
+        if k == MIXED[-1]:
             root = jnp.broadcast_to(lax.rsqrt(square / d + 1e-06), (toks, LANES))
             high = root.astype(BF16).astype(F32)
             lane = lax.broadcasted_iota(jnp.int32, (toks, LANES), 1)
-            gath[k, core, chip, :, pl.ds(kd, LANES)] = jnp.where(
+            gath[k, core, 0, :, pl.ds(kd, LANES)] = jnp.where(
                 lane == 0, high, jnp.where(lane == 1, root - high, 0.0)).astype(BF16)
         for way in range(2):
-            gather_copy(way, 1, k, chip).start()
-        pass_on(chip, k)
+            gather_copy(way, 1, k).start()
+        pass_on(0, k)
 
     other = me + 1 - 2 * core
 
-    def project(k):
-        block = blocks_of(k, 1 - core, slice(None))
-        remote(block, block, fwd_sem.at[0, k], fwd_sem.at[1, k], partner).wait_recv()
-        rows = gath[k, :, :, :, pl.ds(0, kd)].reshape(length, kd)
-        terms = jnp.dot(rows, w[k * kd:(k + 1) * kd, :], preferred_element_type=F32)
-        qkv[...] = terms if k == 0 else qkv[...] + terms
+    def project(k, part_of, fresh):
+        span = spans[part_of]
+        count = span.stop - span.start
+
+        def add(ref, index, rows, cols):
+            rows = rows.reshape(-1, kd)
+            terms = jnp.dot(rows, w[k * kd:(k + 1) * kd, cols], preferred_element_type=F32)
+            terms = terms.reshape(ref[index].shape)
+            ref[index] = terms if fresh else ref[index] + terms
+
+        add(qs, span, gath[k, core, span, :, pl.ds(0, kd)], slice(0, 2 * hd))
+        block = blocks_of(k, 1 - core, pl.ds(span.start, count))
+        remote(block, block, fwd_sem.at[0, k], fwd_sem.at[1 + part_of, k], partner).wait_recv()
+        add(kvs, (slice(None), span), gath[k, :, span, :, pl.ds(0, kd)], slice(2 * hd, 4 * hd))
 
     def send_block(peer):
         remote(sacc.at[peer], racc.at[me], blk_sem.at[0], blk_sem.at[1], {"dp": peer}).start()
@@ -208,59 +230,83 @@
             for c in range(2):
                 send_block(2 * chip_at(pos + step_of[way] * hop) + (core + c) % 2)
 
-    send_block(other)
+    loads["rot"].wait()
+    for j in range(chips):
+        place = chip_at(pos + (j + 1) // 2 * (1 - 2 * (j % 2)))
+        for c in range(2):
+            for t in range(2):
+                turn[t, c, j] = rot[t, place, c]
+
+    half = CHUNKS // 2
+    quarter = n_dp // 8
     for hop in range(1, far + 1):
-        for k in range(CHUNKS):
+        order = AHEAD if hop == 1 else SORTED
+        for i in range(CHUNKS if hop < far else half):
             for way in range(2):
-                if hop > hops(way, k):
-                    continue
-                place = chip_at(pos - step_of[way] * hop)
-                gather_copy(way, hop, k, place).wait_recv()
+                k = order[way][i]
+                gather_copy(way, hop, k).wait_recv()
                 if hop < hops(way, k):
-                    gather_copy(way, hop + 1, k, place).start()
-                pass_on(place, k)
-            if hop == far and k == 0:
+                    gather_copy(way, hop + 1, k).start()
+                pass_on(slot(way, hop), k)
+            if hop == 1:
+                rows = pl.ds(i * kd, kd)
+                share(w.at[rows, kv_cols], w_sem)
+                share(w.at[rows, q_cols], wq_sem)
+                if i < 4:
+                    lax.fori_loop((4 + i) * quarter, (5 + i) * quarter, pack, 0)
+                elif i == 4:
+                    racc[me] = sacc[me]
+                    send_block(other)
+            if hop == 2:
+                share(wo.at[wo_rows, pl.ds(i * kd, kd)], wo_sem)
+            if hop == far - 1 and i == 1:
                 kv_copy.wait_recv()
-                loads["wq"].wait()
-            elif hop == far:
-                project(k - 1)
+                q_copy.wait_recv()
+            if hop == far - 1 and i > 0:
+                project(i - 1, 0, i == 1)
+            if hop == far and i > 0:
+                project(i - 1, 1, i == 1)
+                project(half + i - 1, 1, False)
         if hop == far - 1:
             send_blocks([(way, h) for h in range(1, far) for way in range(2)])
+            project(CHUNKS - 1, 0, False)
     send_blocks([(0, far)])
-    project(CHUNKS - 1)
-
-    loads["rot"].wait()
-    parts = gath[CHUNKS - 1, :, :, :, pl.ds(kd, LANES)].reshape(length, LANES).astype(F32)
-    root = jnp.sum(parts, axis=-1, keepdims=True)
-    cosine, sine = rot[0] * root, rot[1] * root
-
-    def turned(v):
-        return (v * cosine + pltpu.roll(v, hd // 2, 1) * sine).astype(BF16)
-
-    def token_at(shape, dim):
-        row = lax.broadcasted_iota(jnp.int32, shape, dim)
+    project(half - 1, 1, False)
+    project(CHUNKS - 1, 1, False)
+
+    def root_of(parts):
+        return jnp.sum(parts.reshape(-1, LANES).astype(F32), axis=-1, keepdims=True)
+
+    def turned(v, tables, root):
+        return (v * (tables[0].reshape(-1, hd) * root) + pltpu.roll(v, hd // 2, 1) * (tables[1].reshape(-1, hd) * root)).astype(BF16)
+
+    mine = chips * toks
+    root = root_of(gath[CHUNKS - 1, :, :, :, pl.ds(kd, LANES)])
+    own_root = root_of(gath[CHUNKS - 1, core, :, :, pl.ds(kd, LANES)])
+    own_turn = turn[0, core], turn[1, core]
+
+    def token_at(row, first_core):
         block = row // toks
-        return (block % chips * 2 + block // chips) * toks + row % toks
-
-    queries = turned(qkv[:, 0:hd])
-    keys = turned(qkv[:, hd:2 * hd])
-    values = (qkv[:, 2 * hd:3 * hd] * root).astype(BF16)
+        j = block % chips
+        p = (pos + (j + 1) // 2 * (1 - 2 * (j % 2)) + 2 * chips) % chips
+        s = p // (chips // 2)
+        return (2 * (2 * (p * (1 - s) + (chips - 1 - p) * s) + s) + first_core + block // chips) * toks + row % toks
+
+    q_rows = qs[...].reshape(mine, 2 * hd)
+    kv_rows = kvs[...].reshape(length, 2 * hd)
+    queries = jnp.concatenate([turned(q_rows[:, 0:hd], own_turn, own_root), turned(q_rows[:, hd:2 * hd], own_turn, own_root)], axis=0)
+    keys = turned(kv_rows[:, 0:hd], (turn[0], turn[1]), root)
+    values = (kv_rows[:, hd:2 * hd] * root).astype(BF16)
     scores = lax.dot_general(queries, keys, (((1,), (1,)), ((), ())), preferred_element_type=F32)
     scores = scores * ((d / n_dp) ** (-0.5) / 50.0)
-    expd = jnp.where(token_at((1, length), 1) <= token_at((length, 1), 0), jnp.exp(50.0 * jnp.tanh(scores)), 0.0)
+    query_token = token_at(lax.broadcasted_iota(jnp.int32, (2 * mine, 1), 0) % mine, core)
+    key_token = token_at(lax.broadcasted_iota(jnp.int32, (1, length), 1), 0)
+    expd = jnp.where(key_token <= query_token, jnp.exp(50.0 * jnp.tanh(scores)), 0.0)
     denominator = jnp.sum(expd, axis=-1, keepdims=True)
     numer = jnp.dot(expd.astype(BF16), values, preferred_element_type=F32)
     attended = (numer / denominator).astype(BF16)
-
-    att[...] = attended.reshape(2, chips, toks, hd)
-    att_copy = remote(att.at[1 - core], att_in, att_sem.at[0], att_sem.at[1], partner)
-    att_copy.start()
+    both = jnp.concatenate([attended[0:mine], attended[mine:2 * mine]], axis=1)
     wo_copy.wait_recv()
-    ours = att[core].reshape(chips * toks, hd)
-    att_copy.wait_recv()
-    theirs = att_in[...].reshape(chips * toks, hd)
-    even = core == 0
-    both = jnp.concatenate([jnp.where(even, ours, theirs), jnp.where(even, theirs, ours)], axis=1)
 
     def ring_copy(way, step, k):
         return remote(ring_out.at[k, way * far + step - 1], ring_in.at[k, way * far + step - 1],
@@ -270,7 +316,7 @@
         terms = jnp.dot(both, wo[:, k * kd:(k + 1) * kd], preferred_element_type=F32)
         part[k] = terms.reshape(chips, toks, kd)
         for way in range(2):
-            ring_out[k, way * far] = part[k, chip_at(pos + step_of[way] * hops(way, k))].astype(BF16)
+            ring_out[k, way * far] = part[k, slot(1 - way, hops(way, k))].astype(BF16)
             ring_copy(way, 1, k).start()
     for j in range(mb):
         owner, number = origin(secs, sec, mb, act_pp, j)
@@ -297,13 +343,13 @@
                 if left < 1:
                     continue
                 ring_copy(way, step, k).wait_recv()
-                total = part[k, chip_at(pos + step_of[way] * left)] + ring_in[k, way * far + step - 1].astype(F32)
+                total = part[k, slot(1 - way, left)] + ring_in[k, way * far + step - 1].astype(F32)
                 ring_out[k, way * far + step] = total.astype(BF16)
                 ring_copy(way, step + 1, k).start()
 
     pieces = []
     for k in range(CHUNKS):
-        total = part[k, chip_at(pos)]
+        total = part[k, 0]
         for way in range(2):
             step = hops(way, k)
             ring_copy(way, step, k).wait_recv()
@@ -317,7 +363,7 @@
         outbuf[0, :, cols] = (
             moved[0, :, cols].astype(F32) + pieces[k] * scale * post[:, cols]
         ).astype(BF16)
-    for copy in (kv_copy, wo_copy, att_copy, all_blocks):
+    for copy in (kv_copy, q_copy, wo_copy, all_blocks):
         copy.wait_send()
     for o in range(1, n_sec):
         q = (sec + o) % n_sec
@@ -348,8 +394,7 @@
         blk, brows, _ = accumulators.shape
         hd = query_weight.shape[2]
         chips, far, kd, length = n_dp // 2, n_dp // 4, d // CHUNKS, n_dp * toks
-        order = np.arange(length).reshape(chips, 2, toks).transpose(1, 0, 2).reshape(-1)
-        rot = jnp.asarray(rotary_tables(length, hd)[:, order])
+        rot = jnp.asarray(rotary_tables(length, hd).reshape(2, chips, 2, toks, hd))
         smem = pltpu.SMEM
         in_hbm = pl.BlockSpec(memory_space=pltpu.HBM)
         vmem = pl.BlockSpec(memory_space=pltpu.VMEM)
@@ -374,16 +419,16 @@
                 pltpu.VMEM((1, d), F32),
                 pltpu.VMEM((1, d), F32),
                 pltpu.VMEM(rot.shape, F32),
-                pltpu.VMEM((d, 3 * hd), BF16),
+                pltpu.VMEM((2, 2, chips, toks, hd), F32),
+                pltpu.VMEM((d, 4 * hd), BF16),
                 pltpu.VMEM((2 * hd, d), BF16),
                 pltpu.VMEM((n_sec, CHUNKS, act_pp, toks, kd), BF16),
                 (pltpu.VMEM((n_sec, act_pp, toks, kd), BF16),) * CHUNKS,
                 pltpu.VMEM((n_dp, blk_pp, brows, d + LANES), BF16),
                 pltpu.VMEM((n_dp, blk_pp, brows, d + LANES), BF16),
                 pltpu.VMEM((CHUNKS, 2, chips, toks, kd + LANES), BF16),
-                pltpu.VMEM((length, 3 * hd), F32),
-                pltpu.VMEM((2, chips, toks, hd), BF16),
-                pltpu.VMEM((chips, toks, hd), BF16),
+                pltpu.VMEM((chips, toks, 2 * hd), F32),
+                pltpu.VMEM((2, chips, toks, 2 * hd), F32),
                 pltpu.VMEM((CHUNKS, chips, toks, kd), F32),
                 pltpu.VMEM((CHUNKS, 2 * far, toks, kd), BF16),
                 pltpu.VMEM((CHUNKS, 2 * far, toks, kd), BF16),
@@ -393,10 +438,10 @@
                 dma((2,)),
                 dma((2,)),
                 dma((2,)),
+                dma((2,)),
                 dma((CHUNKS,)),
                 dma((2, far, CHUNKS)),
-                dma((2, CHUNKS)),
-                dma((2,)),
+                dma((3, CHUNKS)),
                 dma((CHUNKS,)),
                 dma((2, far, CHUNKS)),
             ],

time: 45.4 us -> 45.4 us (level)
  no operation moved by 1% of the time
where the time goes in v1:
time: 45.4 us; the launch traced here: 45.2 us
  Pallas kernels  44 us (97%)
  between operations  1.29 us (3%)
    pallas_call x1, Pallas kernels, on_device(): pl.pallas_call(functools.partial(kernel, (n_sec, n_dp)), out_shape=(pltpu...  43 us
    pallas_call x1, Pallas kernels, on_device(): pl.pallas_call(write_out, out_shape=(jax.ShapeDtypeStruct(activations.sha...  0.98 us

profile of v1, /device:TPU:0, one launch (start us, length us, event | category | flops | bytes accessed | tf_op | source)
XLA Modules:
  0.0 45.2 jit_solution(6369883710198899249)
XLA Ops:
  1.3 43.0 %shard_map.130 = (bf16[2,16,4608]{2,1,0:T(8,128)(2,1)S(1)}, f32[16,2,4608]{2,1,0:T(2,128)S(1)}, bf16[1,16,4608]{2,1,0:T(8,128)(2,1)S(1)}) custom-call(s32[4]{0:T(128)} %secs_hbm.1, s32[256]{0:T(256)} %blks_hbm.1, f32[1,1]{1,0:T(1,128)S(6)} %copy.14.loss_hbm, bf16[2,16,4608]{2,1,0:T(8,128)(2,1)} %act_hbm.1, f32[16,2,4608]{2,1,0:T(2,128)} %acc_hbm.1, ...), custom_call_target="tpu_custom_call" | custom-call | tf_op jit(solution)/shard_map/pallas_call | solution.py:404
  44.3 1.0 %shard_map.131 = (bf16[2,16,4608]{2,1,0:T(8,128)(2,1)}, f32[16,2,4608]{2,1,0:T(2,128)}, bf16[1,16,4608]{2,1,0:T(8,128)(2,1)}) custom-call(bf16[2,16,4608]{2,1,0:T(8,128)(2,1)S(1)} %get-tuple-element.6.moved, f32[16,2,4608]{2,1,0:T(2,128)S(1)} %get-tuple-element.7.accout, bf16[1,16,4608]{2,1,0:T(8,128)(2,1)S(1)} %get-tuple-element.8.outbuf), custom_call_target="tpu_custom_call" | custom-call | tf_op jit(solution)/shard_map/pallas_call | solution.py:453

commit v2 on v1

--- a/solution.py
+++ b/solution.py
@@ -84,6 +84,9 @@
         return {"dp": 2 * chip_at(p) + core}
 
     partner = {"dp": me + 1 - 2 * core}
+    mate = {"dp": 2 * (2 * rung + 1 - side) + core}
+    cross = far // 2
+    from_middle = ((pos == cross) | (pos == chips - cross), (pos == cross - 1) | (pos == chips - cross - 1))
 
     def remote(src, dst, send_sem, recv_sem, dev):
         return pltpu.make_async_remote_copy(
@@ -95,7 +98,7 @@
     for o in range(1, n_sec):
         pl.semaphore_signal(barrier, inc=1, device_id={"section": (sec + o) % n_sec},
                             device_id_type=pl.DeviceIdType.MESH)
-    for near in (device(pos + 1), device(pos - 1), partner):
+    for near in (device(pos + 1), device(pos - 1), partner, mate):
         pl.semaphore_signal(barrier, inc=1, device_id=near, device_id_type=pl.DeviceIdType.MESH)
 
     kv_cols = pl.ds(pl.multiple_of(2 * hd + core * hd, LANES), hd)
@@ -121,7 +124,7 @@
             block = act[pick(secs, sec, n_sec, mb, q, r)]
             for k in range(CHUNKS):
                 stage[q, k, r] = block[:, k * kd:(k + 1) * kd]
-    pl.semaphore_wait(barrier, n_sec - 1 + 3)
+    pl.semaphore_wait(barrier, n_sec - 1 + 4)
     act_copies = [[] for _ in range(CHUNKS)]
     for k in MIXED:
         for o in range(1, n_sec):
@@ -179,6 +182,18 @@
     def gather_copy(way, hop, k):
         return remote(blocks_of(k, core, slot(way, hop - 1)), blocks_of(k, core, slot(way, hop)),
                       ag_out.at[k], ag_sem.at[way, hop - 1, k], device(pos + step_of[way]))
+
+    def forward(way, hop, k):
+        if hop < hops(way, k):
+            if hop < cross:
+                gather_copy(way, hop + 1, k).start()
+            else:
+                pl.when(jnp.logical_not(from_middle[1 - way]))(gather_copy(way, hop + 1, k).start)
+        there = far + 1 - hop
+        if cross < there <= hops(1 - way, k):
+            across = remote(blocks_of(k, core, slot(way, hop)), blocks_of(k, core, slot(1 - way, there)),
+                            ag_out.at[k], ag_sem.at[1 - way, there - 1, k], mate)
+            pl.when(from_middle[way])(across.start)
 
     near = 2 * (far - 2) + 1
     spans = (slice(0, near), slice(near, chips))
@@ -240,13 +255,12 @@
     half = CHUNKS // 2
     quarter = n_dp // 8
     for hop in range(1, far + 1):
-        order = AHEAD if hop == 1 else SORTED
+        order = (MIXED, MIXED) if hop == 1 else AHEAD if hop < far else SORTED
         for i in range(CHUNKS if hop < far else half):
             for way in range(2):
                 k = order[way][i]
                 gather_copy(way, hop, k).wait_recv()
-                if hop < hops(way, k):
-                    gather_copy(way, hop + 1, k).start()
+                forward(way, hop, k)
                 pass_on(slot(way, hop), k)
             if hop == 1:
                 rows = pl.ds(i * kd, kd)
@@ -259,6 +273,8 @@
                     send_block(other)
             if hop == 2:
                 share(wo.at[wo_rows, pl.ds(i * kd, kd)], wo_sem)
+            if hop == far - 1 and i == CHUNKS - 1:
+                send_blocks([(way, far - h) for h in range(1, far) for way in range(2)])
             if hop == far - 1 and i == 1:
                 kv_copy.wait_recv()
                 q_copy.wait_recv()
@@ -267,10 +283,10 @@
             if hop == far and i > 0:
                 project(i - 1, 1, i == 1)
                 project(half + i - 1, 1, False)
+            if hop == far and i == 0:
+                send_blocks([(0, far)])
         if hop == far - 1:
-            send_blocks([(way, h) for h in range(1, far) for way in range(2)])
             project(CHUNKS - 1, 0, False)
-    send_blocks([(0, far)])
     project(half - 1, 1, False)
     project(CHUNKS - 1, 1, False)
 
@@ -309,19 +325,69 @@
     wo_copy.wait_recv()
 
     def ring_copy(way, step, k):
+        goal = device(pos + step_of[way])
+        if hops(way, k) - step + 1 > cross:
+            goal = {"dp": jnp.where(from_middle[1 - way], mate["dp"], goal["dp"])}
         return remote(ring_out.at[k, way * far + step - 1], ring_in.at[k, way * far + step - 1],
-                      ring_done.at[k], ring_sem.at[way, step - 1, k], device(pos + step_of[way]))
-
-    for k in range(CHUNKS):
+                      ring_done.at[k], ring_sem.at[way, step - 1, k], goal)
+
+    def launch(way, step, k, total):
+        ring_out[k, way * far + step - 1] = total.astype(BF16)
+        ring_copy(way, step, k).start()
+
+    for k in MIXED:
         terms = jnp.dot(both, wo[:, k * kd:(k + 1) * kd], preferred_element_type=F32)
         part[k] = terms.reshape(chips, toks, kd)
+        way = 0 if hops(0, k) == far else 1
+        launch(way, 1, k, part[k, chips - 1])
+    for j in range(half):
         for way in range(2):
-            ring_out[k, way * far] = part[k, slot(1 - way, hops(way, k))].astype(BF16)
-            ring_copy(way, 1, k).start()
+            k = SORTED[way][half + j]
+            launch(way, 1, k, part[k, slot(1 - way, hops(way, k))])
     for j in range(mb):
         owner, number = origin(secs, sec, mb, act_pp, j)
         for k in range(CHUNKS):
             moved[j, :, k * kd:(k + 1) * kd] = actrecv[k][owner, number]
+
+    waited, early = set(), set()
+
+    def take(way, step, k):
+        copy = ring_copy(way, step, k)
+        if (way, step, k) in early:
+            pl.when(jnp.logical_not(from_middle[way]))(copy.wait_recv)
+        else:
+            copy.wait_recv()
+        waited.add((way, step, k))
+        return ring_in[k, way * far + step - 1].astype(F32)
+
+    def relay(way, step, k):
+        left = hops(way, k) - step
+        came = take(way, step, k)
+        if left + 1 > cross:
+            came = jnp.where(from_middle[way], 0.0, came)
+        target = slot(1 - way, left)
+        there = far + 1 - left
+        if cross < there <= hops(1 - way, k):
+            other_step = hops(1 - way, k) - there + 1
+            late = (1 - way, other_step, k) not in waited
+            if late:
+                early.add((1 - way, other_step, k))
+
+            @pl.when(from_middle[1 - way])
+            def _():
+                if late:
+                    ring_copy(1 - way, other_step, k).wait_recv()
+                part[k, target] = part[k, target] + ring_in[k, (1 - way) * far + other_step - 1].astype(F32)
+
+        launch(way, step + 1, k, part[k, target] + came)
+
+    for step in range(1, far):
+        for group in range(2):
+            for j in range(half):
+                for way in range(2):
+                    k = SORTED[way][group * half + j]
+                    if step < hops(way, k):
+                        relay(way, step, k)
 
     others = pl.ds(0, n_dp - 1)
     all_blocks = remote(sacc.at[others], racc.at[others], blk_sem.at[0], blk_sem.at[1], partner)
@@ -336,24 +402,11 @@
 
     lax.fori_loop(0, blk, unpack, 0)
 
-    for step in range(1, far):
-        for k in range(CHUNKS):
-            for way in range(2):
-                left = hops(way, k) - step
-                if left < 1:
-                    continue
-                ring_copy(way, step, k).wait_recv()
-                total = part[k, slot(1 - way, left)] + ring_in[k, way * far + step - 1].astype(F32)
-                ring_out[k, way * far + step] = total.astype(BF16)
-                ring_copy(way, step + 1, k).start()
-
     pieces = []
     for k in range(CHUNKS):
         total = part[k, 0]
         for way in range(2):
-            step = hops(way, k)
-            ring_copy(way, step, k).wait_recv()
-            total = total + ring_in[k, way * far + step - 1].astype(F32)
+            total = total + take(way, hops(way, k), k)
         pieces.append(total)
     loads["post"].wait()
     square = sum(jnp.sum(t * t, axis=-1, keepdims=True) for t in pieces)

time: 45.4 us -> 44.2 us (0.974)
  Pallas kernels: 44 us -> 42.8 us
    pallas_call x1, Pallas kernels: 43 us -> 41.8 us  [on_device(): pl.pallas_call(functools.partial(kernel, (n_sec, n_dp)), out_shape=(pltpu...]
where the time goes in v2:
time: 44.2 us; the launch traced here: 44.1 us
  Pallas kernels  42.8 us (97%)
  between operations  1.29 us (3%)
    pallas_call x1, Pallas kernels, on_device(): pl.pallas_call(functools.partial(kernel, (n_sec, n_dp)), out_shape=(pltpu...  41.8 us
    pallas_call x1, Pallas kernels, on_device(): pl.pallas_call(write_out, out_shape=(jax.ShapeDtypeStruct(activations.sha...  0.98 us

profile of v2, /device:TPU:0, one launch (start us, length us, event | category | flops | bytes accessed | tf_op | source)
XLA Modules:
  0.0 44.1 jit_solution(2305576522297353838)
XLA Ops:
  1.3 41.8 %shard_map.130 = (bf16[2,16,4608]{2,1,0:T(8,128)(2,1)S(1)}, f32[16,2,4608]{2,1,0:T(2,128)S(1)}, bf16[1,16,4608]{2,1,0:T(8,128)(2,1)S(1)}) custom-call(s32[4]{0:T(128)} %secs_hbm.1, s32[256]{0:T(256)} %blks_hbm.1, f32[1,1]{1,0:T(1,128)S(6)} %copy.14.loss_hbm, bf16[2,16,4608]{2,1,0:T(8,128)(2,1)} %act_hbm.1, f32[16,2,4608]{2,1,0:T(2,128)} %acc_hbm.1, ...), custom_call_target="tpu_custom_call" | custom-call | tf_op jit(solution)/shard_map/pallas_call | solution.py:457
  43.1 1.0 %shard_map.131 = (bf16[2,16,4608]{2,1,0:T(8,128)(2,1)}, f32[16,2,4608]{2,1,0:T(2,128)}, bf16[1,16,4608]{2,1,0:T(8,128)(2,1)}) custom-call(bf16[2,16,4608]{2,1,0:T(8,128)(2,1)S(1)} %get-tuple-element.6.moved, f32[16,2,4608]{2,1,0:T(2,128)S(1)} %get-tuple-element.7.accout, bf16[1,16,4608]{2,1,0:T(8,128)(2,1)S(1)} %get-tuple-element.8.outbuf), custom_call_target="tpu_custom_call" | custom-call | tf_op jit(solution)/shard_map/pallas_call | solution.py:506

commit v3 on v2

--- a/solution.py
+++ b/solution.py
@@ -56,10 +56,10 @@
     dims,
     secs_hbm, blks_hbm, loss_hbm, act_hbm, acc_hbm, pre_hbm, wq_hbm, wkv_hbm, wo_hbm, post_hbm, rot_hbm,
     moved, accout, outbuf,
-    secs, blks, loss, act, acc, pre, post, rot, turn, w, wo,
+    secs, blks, loss, act, acc, pre, post, rot, turn, seen, w, wo,
     stage, actrecv, sacc, racc,
     gath, qs, kvs, part, ring_in, ring_out,
-    load_sem, act_out, act_sem, w_sem, wq_sem, wo_sem, blk_sem, ag_out, ag_sem, fwd_sem, ring_done, ring_sem,
+    ready, load_sem, act_out, act_sem, w_sem, blk_sem, ag_out, ag_sem, fwd_out, fwd_sem, ring_done, ring_sem,
 ):
     n_sec, n_dp = dims
     mb, toks, d = act.shape
@@ -81,10 +81,10 @@
         return 2 * (q * (1 - s) + (chips - 1 - q) * s) + s
 
     def device(p):
-        return {"dp": 2 * chip_at(p) + core}
+        return {"dp": 2 * chip_at(p) + 1 - core}
 
     partner = {"dp": me + 1 - 2 * core}
-    mate = {"dp": 2 * (2 * rung + 1 - side) + core}
+    mate = {"dp": 2 * (2 * rung + 1 - side) + 1 - core}
     cross = far // 2
     from_middle = ((pos == cross) | (pos == chips - cross), (pos == cross - 1) | (pos == chips - cross - 1))
 
@@ -98,23 +98,26 @@
     for o in range(1, n_sec):
         pl.semaphore_signal(barrier, inc=1, device_id={"section": (sec + o) % n_sec},
                             device_id_type=pl.DeviceIdType.MESH)
-    for near in (device(pos + 1), device(pos - 1), partner, mate):
+    def same(dev):
+        return {"dp": dev["dp"] + 2 * core - 1}
+
+    for near in (same(device(pos + 1)), same(device(pos - 1)), partner, same(mate)):
         pl.semaphore_signal(barrier, inc=1, device_id=near, device_id_type=pl.DeviceIdType.MESH)
 
     kv_cols = pl.ds(pl.multiple_of(2 * hd + core * hd, LANES), hd)
     q_cols = pl.ds(pl.multiple_of(core * hd, LANES), hd)
     wo_rows = pl.ds(pl.multiple_of(core * hd, LANES), hd)
-    names = ("secs", "act", "pre", "wkv", "wo", "blks", "loss", "acc", "wq", "rot", "post")
+    names = ("secs", "act", "pre", "wkv", "blks", "loss", "acc", "rot", "post", "wo", "wq")
     pairs = [
         (secs_hbm, secs), (act_hbm, act), (pre_hbm, pre), (wkv_hbm.at[0], w.at[:, kv_cols]),
-        (wo_hbm.at[0], wo.at[wo_rows]), (blks_hbm, blks), (loss_hbm, loss), (acc_hbm, acc),
-        (wq_hbm.at[0], w.at[:, q_cols]), (rot_hbm, rot), (post_hbm, post),
+        (blks_hbm, blks), (loss_hbm, loss), (acc_hbm, acc), (rot_hbm, rot), (post_hbm, post),
+        (wo_hbm.at[0], wo.at[wo_rows]), (wq_hbm.at[0], w.at[:, q_cols]),
     ]
     loads = {
-        name: pltpu.make_async_copy(src, dst, load_sem.at[i])
+        name: pltpu.make_async_copy(src, dst, load_sem.at[names.index("wkv") if name in ("wq", "wo") else i])
         for i, (name, (src, dst)) in enumerate(zip(names, pairs))
     }
-    for name in names:
+    for name in ("secs", "act", "wkv", "wq", "wo", "pre", "blks", "loss", "acc", "rot", "post"):
         loads[name].start()
 
     loads["secs"].wait()
@@ -125,6 +128,7 @@
             for k in range(CHUNKS):
                 stage[q, k, r] = block[:, k * kd:(k + 1) * kd]
     pl.semaphore_wait(barrier, n_sec - 1 + 4)
+    pl.semaphore_signal(ready, inc=1, device_id=partner, device_id_type=pl.DeviceIdType.MESH)
     act_copies = [[] for _ in range(CHUNKS)]
     for k in MIXED:
         for o in range(1, n_sec):
@@ -135,18 +139,28 @@
     for k in range(CHUNKS):
         actrecv[k][sec] = stage[sec, k]
 
-    loads["wkv"].wait()
-    loads["wo"].wait()
-    loads["wq"].wait()
-
-    def whole(ref, sems):
-        return remote(ref, ref, sems.at[0], sems.at[1], partner)
-
-    kv_copy, q_copy = whole(w.at[:, kv_cols], w_sem), whole(w.at[:, q_cols], wq_sem)
-    wo_copy = whole(wo.at[wo_rows], wo_sem)
-
-    def share(ref, sems):
-        remote(ref, ref, sems.at[0], sems.at[1], partner).start()
+    mine = chips * toks
+
+    def token_at(row, first_core):
+        block = row // toks
+        j = block % chips
+        p = (pos + (j + 1) // 2 * (1 - 2 * (j % 2)) + 2 * chips) % chips
+        s = p // (chips // 2)
+        return (2 * (2 * (p * (1 - s) + (chips - 1 - p) * s) + s) + (first_core + block // chips + (j + 1) // 2) % 2) * toks + row % toks
+
+    query_token = token_at(lax.broadcasted_iota(jnp.int32, (2 * mine, 1), 0) % mine, core)
+    key_token = token_at(lax.broadcasted_iota(jnp.int32, (1, length), 1), 0)
+    seen[...] = (key_token <= query_token).astype(F32)
+
+    three = w.at[:, pl.ds(0, 3 * hd)]
+    weights_loaded = load_sem.at[names.index("wkv")]
+    remote(three, three, weights_loaded, weights_loaded, partner).wait_recv()
+    two = w.at[:, pl.ds(0, 2 * hd)]
+    weights = remote(two, two, w_sem.at[0], w_sem.at[1], partner)
+    wo_copy = remote(wo.at[wo_rows], wo.at[wo_rows], w_sem.at[2], w_sem.at[3], partner)
+
+    def share(ref, i):
+        remote(ref, ref, w_sem.at[i], w_sem.at[i + 1], partner).start()
 
     for name in ("acc", "blks", "loss"):
         loads[name].wait()
@@ -173,6 +187,12 @@
     def width(k):
         return kd + LANES if k == MIXED[-1] else kd
 
+    def place_of(way, hop, k):
+        return (hop - 1) * 2 * CHUNKS + (way * CHUNKS if hop < far else 0) + k
+
+    def last(k):
+        return 1 if k == MIXED[-1] else 0
+
     def slot(way, hop):
         return 0 if hop == 0 else min(2 * hop - 1 + way, chips - 1)
 
@@ -180,8 +200,8 @@
         return gath.at[k, c, slots, :, pl.ds(0, width(k))]
 
     def gather_copy(way, hop, k):
-        return remote(blocks_of(k, core, slot(way, hop - 1)), blocks_of(k, core, slot(way, hop)),
-                      ag_out.at[k], ag_sem.at[way, hop - 1, k], device(pos + step_of[way]))
+        return remote(blocks_of(k, core, slot(way, hop - 1)), blocks_of(k, 1 - core, slot(way, hop)),
+                      ag_out.at[last(k)], ag_sem.at[place_of(way, hop, k)], device(pos + step_of[way]))
 
     def forward(way, hop, k):
         if hop < hops(way, k):
@@ -191,8 +211,8 @@
                 pl.when(jnp.logical_not(from_middle[1 - way]))(gather_copy(way, hop + 1, k).start)
         there = far + 1 - hop
         if cross < there <= hops(1 - way, k):
-            across = remote(blocks_of(k, core, slot(way, hop)), blocks_of(k, core, slot(1 - way, there)),
-                            ag_out.at[k], ag_sem.at[1 - way, there - 1, k], mate)
+            across = remote(blocks_of(k, core, slot(way, hop)), blocks_of(k, 1 - core, slot(1 - way, there)),
+                            ag_out.at[last(k)], ag_sem.at[place_of(1 - way, there, k)], mate)
             pl.when(from_middle[way])(across.start)
 
     near = 2 * (far - 2) + 1
@@ -200,8 +220,9 @@
 
     def pass_on(j, k):
         block = blocks_of(k, core, j)
-        remote(block, block, fwd_sem.at[0, k], fwd_sem.at[1 if j < near else 2, k], partner).start()
-
+        remote(block, block, fwd_out.at[last(k)], fwd_sem.at[0 if j < near else 1, k], partner).start()
+
+    pl.semaphore_wait(ready, 1)
     square = jnp.zeros((toks, 1), F32)
     for k in MIXED:
         for copy in act_copies[k]:
@@ -222,20 +243,23 @@
 
     other = me + 1 - 2 * core
 
-    def project(k, part_of, fresh):
+    def project(ks, part_of, fresh):
         span = spans[part_of]
         count = span.stop - span.start
 
-        def add(ref, index, rows, cols):
-            rows = rows.reshape(-1, kd)
-            terms = jnp.dot(rows, w[k * kd:(k + 1) * kd, cols], preferred_element_type=F32)
-            terms = terms.reshape(ref[index].shape)
+        def add(ref, index, cores, cols):
+            terms = sum(
+                jnp.dot(gath[k, cores, span, :, pl.ds(0, kd)].reshape(-1, kd), w[k * kd:(k + 1) * kd, cols],
+                        preferred_element_type=F32)
+                for k in ks
+            ).reshape(ref[index].shape)
             ref[index] = terms if fresh else ref[index] + terms
 
-        add(qs, span, gath[k, core, span, :, pl.ds(0, kd)], slice(0, 2 * hd))
-        block = blocks_of(k, 1 - core, pl.ds(span.start, count))
-        remote(block, block, fwd_sem.at[0, k], fwd_sem.at[1 + part_of, k], partner).wait_recv()
-        add(kvs, (slice(None), span), gath[k, :, span, :, pl.ds(0, kd)], slice(2 * hd, 4 * hd))
+        add(qs, span, core, slice(0, 2 * hd))
+        for k in ks:
+            block = blocks_of(k, 1 - core, pl.ds(span.start, count))
+            remote(block, block, fwd_out.at[0], fwd_sem.at[part_of, k], partner).wait_recv()
+        add(kvs, (slice(None), span), slice(None), slice(2 * hd, 4 * hd))
 
     def send_block(peer):
         remote(sacc.at[peer], racc.at[me], blk_sem.at[0], blk_sem.at[1], {"dp": peer}).start()
@@ -250,7 +274,7 @@
         place = chip_at(pos + (j + 1) // 2 * (1 - 2 * (j % 2)))
         for c in range(2):
             for t in range(2):
-                turn[t, c, j] = rot[t, place, c]
+                turn[t, c, j] = rot[t, place, (c + (j + 1) // 2) % 2]
 
     half = CHUNKS // 2
     quarter = n_dp // 8
@@ -264,31 +288,26 @@
                 pass_on(slot(way, hop), k)
             if hop == 1:
                 rows = pl.ds(i * kd, kd)
-                share(w.at[rows, kv_cols], w_sem)
-                share(w.at[rows, q_cols], wq_sem)
+                share(w.at[rows, kv_cols], 0)
+                share(w.at[rows, q_cols], 0)
                 if i < 4:
                     lax.fori_loop((4 + i) * quarter, (5 + i) * quarter, pack, 0)
                 elif i == 4:
                     racc[me] = sacc[me]
                     send_block(other)
             if hop == 2:
-                share(wo.at[wo_rows, pl.ds(i * kd, kd)], wo_sem)
+                share(wo.at[wo_rows, pl.ds(i * kd, kd)], 2)
             if hop == far - 1 and i == CHUNKS - 1:
                 send_blocks([(way, far - h) for h in range(1, far) for way in range(2)])
             if hop == far - 1 and i == 1:
-                kv_copy.wait_recv()
-                q_copy.wait_recv()
-            if hop == far - 1 and i > 0:
-                project(i - 1, 0, i == 1)
+                weights.wait_recv()
+            if hop == far - 1 and i % 2 == 1:
+                project(MIXED[i - 1:i + 1], 0, i == 1)
             if hop == far and i > 0:
-                project(i - 1, 1, i == 1)
-                project(half + i - 1, 1, False)
+                project((i - 1, half + i - 1), 1, i == 1)
             if hop == far and i == 0:
                 send_blocks([(0, far)])
-        if hop == far - 1:
-            project(CHUNKS - 1, 0, False)
-    project(half - 1, 1, False)
-    project(CHUNKS - 1, 1, False)
+    project((half - 1, CHUNKS - 1), 1, False)
 
     def root_of(parts):
         return jnp.sum(parts.reshape(-1, LANES).astype(F32), axis=-1, keepdims=True)
@@ -296,17 +315,9 @@
     def turned(v, tables, root):
         return (v * (tables[0].reshape(-1, hd) * root) + pltpu.roll(v, hd // 2, 1) * (tables[1].reshape(-1, hd) * root)).astype(BF16)
 
-    mine = chips * toks
     root = root_of(gath[CHUNKS - 1, :, :, :, pl.ds(kd, LANES)])
     own_root = root_of(gath[CHUNKS - 1, core, :, :, pl.ds(kd, LANES)])
     own_turn = turn[0, core], turn[1, core]
-
-    def token_at(row, first_core):
-        block = row // toks
-        j = block % chips
-        p = (pos + (j + 1) // 2 * (1 - 2 * (j % 2)) + 2 * chips) % chips
-        s = p // (chips // 2)
-        return (2 * (2 * (p * (1 - s) + (chips - 1 - p) * s) + s) + first_core + block // chips) * toks + row % toks
 
     q_rows = qs[...].reshape(mine, 2 * hd)
     kv_rows = kvs[...].reshape(length, 2 * hd)
@@ -315,21 +326,19 @@
     values = (kv_rows[:, hd:2 * hd] * root).astype(BF16)
     scores = lax.dot_general(queries, keys, (((1,), (1,)), ((), ())), preferred_element_type=F32)
     scores = scores * ((d / n_dp) ** (-0.5) / 50.0)
-    query_token = token_at(lax.broadcasted_iota(jnp.int32, (2 * mine, 1), 0) % mine, core)
-    key_token = token_at(lax.broadcasted_iota(jnp.int32, (1, length), 1), 0)
-    expd = jnp.where(key_token <= query_token, jnp.exp(50.0 * jnp.tanh(scores)), 0.0)
+    expd = jnp.exp(50.0 * jnp.tanh(scores)) * seen[...]
     denominator = jnp.sum(expd, axis=-1, keepdims=True)
     numer = jnp.dot(expd.astype(BF16), values, preferred_element_type=F32)
     attended = (numer / denominator).astype(BF16)
+    wo_copy.wait_recv()
     both = jnp.concatenate([attended[0:mine], attended[mine:2 * mine]], axis=1)
-    wo_copy.wait_recv()
 
     def ring_copy(way, step, k):
         goal = device(pos + step_of[way])
         if hops(way, k) - step + 1 > cross:
             goal = {"dp": jnp.where(from_middle[1 - way], mate["dp"], goal["dp"])}
         return remote(ring_out.at[k, way * far + step - 1], ring_in.at[k, way * far + step - 1],
-                      ring_done.at[k], ring_sem.at[way, step - 1, k], goal)
+                      ring_done.at[0], ring_sem.at[place_of(way, step, k)], goal)
 
     def launch(way, step, k, total):
         ring_out[k, way * far + step - 1] = total.astype(BF16)
@@ -416,17 +425,17 @@
         outbuf[0, :, cols] = (
             moved[0, :, cols].astype(F32) + pieces[k] * scale * post[:, cols]
         ).astype(BF16)
-    for copy in (kv_copy, q_copy, wo_copy, all_blocks):
+    for copy in (weights, wo_copy, all_blocks):
         copy.wait_send()
     for o in range(1, n_sec):
         q = (sec + o) % n_sec
         remote(stage.at[q], stage.at[q], act_out.at[o - 1], act_sem.at[o - 1, 0], {"section": q}).wait_send()
-    for k in range(CHUNKS):
-        for places, sem in ((slice(None), fwd_sem.at[0, k]), (pl.ds(0, chips - 1), ag_out.at[k])):
-            block = blocks_of(k, core, places)
-            remote(block, block, sem, fwd_sem.at[1, k], partner).wait_send()
-        block = ring_out.at[k, pl.ds(0, chips - 1)]
-        remote(block, block, ring_done.at[k], fwd_sem.at[1, k], partner).wait_send()
+    for i, span in enumerate((pl.ds(0, CHUNKS - 1), pl.ds(CHUNKS - 1, 1))):
+        for slots, sem in ((chips, fwd_out.at[i]), (chips - 1, ag_out.at[i])):
+            block = gath.at[span, core, pl.ds(0, slots), :, pl.ds(0, width(i * (CHUNKS - 1)))]
+            remote(block, block, sem, fwd_sem.at[0, 0], partner).wait_send()
+    block = ring_out.at[:, pl.ds(0, chips - 1)]
+    remote(block, block, ring_done.at[0], fwd_sem.at[0, 0], partner).wait_send()
 
 
 def write_out(moved, accout, outbuf, moved_hbm, newacc_hbm, check_hbm, sems):
@@ -473,6 +482,7 @@
                 pltpu.VMEM((1, d), F32),
                 pltpu.VMEM(rot.shape, F32),
                 pltpu.VMEM((2, 2, chips, toks, hd), F32),
+                pltpu.VMEM((length, length), F32),
                 pltpu.VMEM((d, 4 * hd), BF16),
                 pltpu.VMEM((2 * hd, d), BF16),
                 pltpu.VMEM((n_sec, CHUNKS, act_pp, toks, kd), BF16),
@@ -485,18 +495,18 @@
                 pltpu.VMEM((CHUNKS, chips, toks, kd), F32),
                 pltpu.VMEM((CHUNKS, 2 * far, toks, kd), BF16),
                 pltpu.VMEM((CHUNKS, 2 * far, toks, kd), BF16),
-                dma((11,)),
+                pltpu.SemaphoreType.REGULAR,
+                dma((9,)),
                 dma((n_sec - 1,)),
                 dma((n_sec - 1, CHUNKS)),
+                dma((4,)),
                 dma((2,)),
                 dma((2,)),
+                dma(((2 * far - 1) * CHUNKS,)),
                 dma((2,)),
-                dma((2,)),
-                dma((CHUNKS,)),
-                dma((2, far, CHUNKS)),
-                dma((3, CHUNKS)),
-                dma((CHUNKS,)),
-                dma((2, far, CHUNKS)),
+                dma((2, CHUNKS)),
+                dma((1,)),
+                dma(((2 * far - 1) * CHUNKS,)),
             ],
             compiler_params=pltpu.CompilerParams(
                 collective_id=0, has_side_effects=True, vmem_limit_bytes=VMEM_BYTES - 2**16 - out_bytes

time: 44.2 us -> 42.4 us (0.959)
  Pallas kernels: 42.8 us -> 40.9 us
    pallas_call x1, Pallas kernels: 41.8 us -> 40 us  [on_device(): pl.pallas_call(functools.partial(kernel, (n_sec, n_dp)), out_shape=(pltpu...]
where the time goes in v3:
time: 42.4 us; the launch traced here: 42.2 us
  Pallas kernels  40.9 us (96%)
  between operations  1.29 us (3%)
    pallas_call x1, Pallas kernels, on_device(): pl.pallas_call(functools.partial(kernel, (n_sec, n_dp)), out_shape=(pltpu...  40 us
    pallas_call x1, Pallas kernels, on_device(): pl.pallas_call(write_out, out_shape=(jax.ShapeDtypeStruct(activations.sha...  0.98 us

profile of v3, /device:TPU:0, one launch (start us, length us, event | category | flops | bytes accessed | tf_op | source)
XLA Modules:
  0.0 42.2 jit_solution(4265045874333030313)
XLA Ops:
  1.3 40.0 %shard_map.130 = (bf16[2,16,4608]{2,1,0:T(8,128)(2,1)S(1)}, f32[16,2,4608]{2,1,0:T(2,128)S(1)}, bf16[1,16,4608]{2,1,0:T(8,128)(2,1)S(1)}) custom-call(s32[4]{0:T(128)} %secs_hbm.1, s32[256]{0:T(256)} %blks_hbm.1, f32[1,1]{1,0:T(1,128)S(6)} %copy.14.loss_hbm, bf16[2,16,4608]{2,1,0:T(8,128)(2,1)} %act_hbm.1, f32[16,2,4608]{2,1,0:T(2,128)} %acc_hbm.1, ...), custom_call_target="tpu_custom_call" | custom-call | tf_op jit(solution)/shard_map/pallas_call | solution.py:466
  41.2 1.0 %shard_map.131 = (bf16[2,16,4608]{2,1,0:T(8,128)(2,1)}, f32[16,2,4608]{2,1,0:T(2,128)}, bf16[1,16,4608]{2,1,0:T(8,128)(2,1)}) custom-call(bf16[2,16,4608]{2,1,0:T(8,128)(2,1)S(1)} %get-tuple-element.6.moved, f32[16,2,4608]{2,1,0:T(2,128)S(1)} %get-tuple-element.7.accout, bf16[1,16,4608]{2,1,0:T(8,128)(2,1)S(1)} %get-tuple-element.8.outbuf), custom_call_target="tpu_custom_call" | custom-call | tf_op jit(solution)/shard_map/pallas_call | solution.py:516

commit v4 on v3

--- a/solution.py
+++ b/solution.py
@@ -19,15 +19,17 @@
 
 
 def pick(table, own, groups, per_group, peer, rank):
-    def visit(j, carry):
-        seen, found = carry
-        source = table[peer * per_group + j]
-        mine = (source // per_group == own).astype(jnp.int32)
-        hit = mine * (seen == rank).astype(jnp.int32)
-        return seen + mine, found + hit * (source % per_group)
-
-    zero = jnp.int32(0)
-    return lax.fori_loop(0, per_group, visit, (zero, zero), unroll=True)[1]
+    first, start = peer * per_group, own * per_group
+    seen = found = jnp.int32(0)
+    for j in range(per_group):
+        offset = table[first + j] - start
+        hit = (offset >= 0) & (offset < per_group)
+        if per_group == groups:
+            found = jnp.where(hit, offset, found)
+        else:
+            found = jnp.where(hit & (seen == rank), offset, found)
+            seen = seen + hit.astype(jnp.int32)
+    return found
 
 
 def origin(table, own, per_group, per_peer, entry):
@@ -117,7 +119,7 @@
         name: pltpu.make_async_copy(src, dst, load_sem.at[names.index("wkv") if name in ("wq", "wo") else i])
         for i, (name, (src, dst)) in enumerate(zip(names, pairs))
     }
-    for name in ("secs", "act", "wkv", "wq", "wo", "pre", "blks", "loss", "acc", "rot", "post"):
+    for name in ("secs", "act", "blks", "loss", "acc", "pre", "wkv", "wq", "wo", "rot", "post"):
         loads[name].start()
 
     loads["secs"].wait()
@@ -139,29 +141,6 @@
     for k in range(CHUNKS):
         actrecv[k][sec] = stage[sec, k]
 
-    mine = chips * toks
-
-    def token_at(row, first_core):
-        block = row // toks
-        j = block % chips
-        p = (pos + (j + 1) // 2 * (1 - 2 * (j % 2)) + 2 * chips) % chips
-        s = p // (chips // 2)
-        return (2 * (2 * (p * (1 - s) + (chips - 1 - p) * s) + s) + (first_core + block // chips + (j + 1) // 2) % 2) * toks + row % toks
-
-    query_token = token_at(lax.broadcasted_iota(jnp.int32, (2 * mine, 1), 0) % mine, core)
-    key_token = token_at(lax.broadcasted_iota(jnp.int32, (1, length), 1), 0)
-    seen[...] = (key_token <= query_token).astype(F32)
-
-    three = w.at[:, pl.ds(0, 3 * hd)]
-    weights_loaded = load_sem.at[names.index("wkv")]
-    remote(three, three, weights_loaded, weights_loaded, partner).wait_recv()
-    two = w.at[:, pl.ds(0, 2 * hd)]
-    weights = remote(two, two, w_sem.at[0], w_sem.at[1], partner)
-    wo_copy = remote(wo.at[wo_rows], wo.at[wo_rows], w_sem.at[2], w_sem.at[3], partner)
-
-    def share(ref, i):
-        remote(ref, ref, w_sem.at[i], w_sem.at[i + 1], partner).start()
-
     for name in ("acc", "blks", "loss"):
         loads[name].wait()
     term = jnp.full((brows, LANES), loss[0, 0], F32)
@@ -176,13 +155,44 @@
             sacc[p, r, :, pl.ds(d, LANES)] = tail.astype(BF16)
         return carry
 
-    lax.fori_loop(0, n_dp // 2, pack, 0)
+    def pack_near(i, carry):
+        j = (i // 2 + 1) % chips
+        return pack(2 * chip_at(pos + (j + 1) // 2 * (1 - 2 * (j % 2))) + i % 2, carry)
+
+    other = me + 1 - 2 * core
+    step_of = (1, -1)
+
+    def send_block(peer):
+        remote(sacc.at[peer], racc.at[me], blk_sem.at[0], blk_sem.at[1], {"dp": peer}).start()
+
+    def send_blocks(places):
+        for way, hop in places:
+            for c in range(2):
+                send_block(2 * chip_at(pos + step_of[way] * hop) + (core + c) % 2)
+
+    lax.fori_loop(0, 4, pack_near, 0)
+    pl.semaphore_wait(ready, 1)
+    send_blocks([(0, 1), (1, 1)])
+    some = n_dp // 16
+    lax.fori_loop(4, n_dp - 4 * some, pack_near, 0)
+    mine = chips * toks
+
+    def token_at(row, first_core):
+        block = row // toks
+        j = block % chips
+        p = (pos + (j + 1) // 2 * (1 - 2 * (j % 2)) + 2 * chips) % chips
+        s = p // (chips // 2)
+        return (2 * (2 * (p * (1 - s) + (chips - 1 - p) * s) + s) + (first_core + block // chips + (j + 1) // 2) % 2) * toks + row % toks
+
+    query_token = token_at(lax.broadcasted_iota(jnp.int32, (2 * mine, 1), 0) % mine, core)
+    key_token = token_at(lax.broadcasted_iota(jnp.int32, (1, length), 1), 0)
+    seen[...] = (key_token <= query_token).astype(F32)
+
     loads["pre"].wait()
 
     def hops(way, k):
         return far if (k < CHUNKS // 2) == (way == 0) else far - 1
 
-    step_of = (1, -1)
 
     def width(k):
         return kd + LANES if k == MIXED[-1] else kd
@@ -222,7 +232,6 @@
         block = blocks_of(k, core, j)
         remote(block, block, fwd_out.at[last(k)], fwd_sem.at[0 if j < near else 1, k], partner).start()
 
-    pl.semaphore_wait(ready, 1)
     square = jnp.zeros((toks, 1), F32)
     for k in MIXED:
         for copy in act_copies[k]:
@@ -241,7 +250,6 @@
             gather_copy(way, 1, k).start()
         pass_on(0, k)
 
-    other = me + 1 - 2 * core
 
     def project(ks, part_of, fresh):
         span = spans[part_of]
@@ -261,13 +269,15 @@
             remote(block, block, fwd_out.at[0], fwd_sem.at[part_of, k], partner).wait_recv()
         add(kvs, (slice(None), span), slice(None), slice(2 * hd, 4 * hd))
 
-    def send_block(peer):
-        remote(sacc.at[peer], racc.at[me], blk_sem.at[0], blk_sem.at[1], {"dp": peer}).start()
-
-    def send_blocks(places):
-        for way, hop in places:
-            for c in range(2):
-                send_block(2 * chip_at(pos + step_of[way] * hop) + (core + c) % 2)
+    three = w.at[:, pl.ds(0, 3 * hd)]
+    weights_loaded = load_sem.at[names.index("wkv")]
+    remote(three, three, weights_loaded, weights_loaded, partner).wait_recv()
+    two = w.at[:, pl.ds(0, 2 * hd)]
+    weights = remote(two, two, w_sem.at[0], w_sem.at[1], partner)
+    wo_copy = remote(wo.at[wo_rows], wo.at[wo_rows], w_sem.at[2], w_sem.at[3], partner)
+
+    def share(ref, i):
+        remote(ref, ref, w_sem.at[i], w_sem.at[i + 1], partner).start()
 
     loads["rot"].wait()
     for j in range(chips):
@@ -277,7 +287,6 @@
                 turn[t, c, j] = rot[t, place, (c + (j + 1) // 2) % 2]
 
     half = CHUNKS // 2
-    quarter = n_dp // 8
     for hop in range(1, far + 1):
         order = (MIXED, MIXED) if hop == 1 else AHEAD if hop < far else SORTED
         for i in range(CHUNKS if hop < far else half):
@@ -291,14 +300,14 @@
                 share(w.at[rows, kv_cols], 0)
                 share(w.at[rows, q_cols], 0)
                 if i < 4:
-                    lax.fori_loop((4 + i) * quarter, (5 + i) * quarter, pack, 0)
+                    lax.fori_loop(n_dp - (4 - i) * some, n_dp - (3 - i) * some, pack_near, 0)
                 elif i == 4:
                     racc[me] = sacc[me]
                     send_block(other)
             if hop == 2:
                 share(wo.at[wo_rows, pl.ds(i * kd, kd)], 2)
             if hop == far - 1 and i == CHUNKS - 1:
-                send_blocks([(way, far - h) for h in range(1, far) for way in range(2)])
+                send_blocks([(way, far - h) for h in range(1, far - 1) for way in range(2)])
             if hop == far - 1 and i == 1:
                 weights.wait_recv()
             if hop == far - 1 and i % 2 == 1:
@@ -340,9 +349,16 @@
         return remote(ring_out.at[k, way * far + step - 1], ring_in.at[k, way * far + step - 1],
                       ring_done.at[0], ring_sem.at[place_of(way, step, k)], goal)
 
+    def crossing(way, step, k):
+        return hops(way, k) - step + 1 > cross
+
     def launch(way, step, k, total):
         ring_out[k, way * far + step - 1] = total.astype(BF16)
-        ring_copy(way, step, k).start()
+        start = ring_copy(way, step, k).start
+        if step == 1 and crossing(way, 1, k):
+            pl.when(jnp.logical_not(from_middle[1 - way]))(start)
+        else:
+            start()
 
     for k in MIXED:
         terms = jnp.dot(both, wo[:, k * kd:(k + 1) * kd], preferred_element_type=F32)
@@ -358,37 +374,24 @@
         for k in range(CHUNKS):
             moved[j, :, k * kd:(k + 1) * kd] = actrecv[k][owner, number]
 
-    waited, early = set(), set()
-
     def take(way, step, k):
-        copy = ring_copy(way, step, k)
-        if (way, step, k) in early:
-            pl.when(jnp.logical_not(from_middle[way]))(copy.wait_recv)
-        else:
-            copy.wait_recv()
-        waited.add((way, step, k))
+        ring_copy(way, step, k).wait_recv()
         return ring_in[k, way * far + step - 1].astype(F32)
 
     def relay(way, step, k):
         left = hops(way, k) - step
-        came = take(way, step, k)
-        if left + 1 > cross:
-            came = jnp.where(from_middle[way], 0.0, came)
         target = slot(1 - way, left)
         there = far + 1 - left
+        if crossing(way, step, k):
+            @pl.when(jnp.logical_not(from_middle[way]))
+            def _():
+                part[k, target] = part[k, target] + take(way, step, k)
         if cross < there <= hops(1 - way, k):
-            other_step = hops(1 - way, k) - there + 1
-            late = (1 - way, other_step, k) not in waited
-            if late:
-                early.add((1 - way, other_step, k))
-
             @pl.when(from_middle[1 - way])
             def _():
-                if late:
-                    ring_copy(1 - way, other_step, k).wait_recv()
-                part[k, target] = part[k, target] + ring_in[k, (1 - way) * far + other_step - 1].astype(F32)
-
-        launch(way, step + 1, k, part[k, target] + came)
+                part[k, target] = part[k, target] + take(1 - way, hops(1 - way, k) - there + 1, k)
+        total = part[k, target]
+        launch(way, step + 1, k, total if crossing(way, step, k) else total + take(way, step, k))
 
     for step in range(1, far):
         for group in range(2):
@@ -397,6 +400,10 @@
                     k = SORTED[way][group * half + j]
                     if step < hops(way, k):
                         relay(way, step, k)
+            if step == 1 and group == 0:
+                for way in range(2):
+                    for k in SORTED[way][half:] + SORTED[way][:half]:
+                        pl.when(from_middle[1 - way])(ring_copy(way, 1, k).start)
 
     others = pl.ds(0, n_dp - 1)
     all_blocks = remote(sacc.at[others], racc.at[others], blk_sem.at[0], blk_sem.at[1], partner)

time: 42.4 us -> 41.7 us (0.983)
  Pallas kernels: 40.9 us -> 40.2 us
    pallas_call x1, Pallas kernels: 40 us -> 39.2 us  [on_device(): pl.pallas_call(functools.partial(kernel, (n_sec, n_dp)), out_shape=(pltpu...]
where the time goes in v4:
time: 41.7 us; the launch traced here: 41.5 us
  Pallas kernels  40.2 us (96%)
  between operations  1.29 us (3%)
    pallas_call x1, Pallas kernels, on_device(): pl.pallas_call(functools.partial(kernel, (n_sec, n_dp)), out_shape=(pltpu...  39.2 us
    pallas_call x1, Pallas kernels, on_device(): pl.pallas_call(write_out, out_shape=(jax.ShapeDtypeStruct(activations.sha...  0.98 us

profile of v4, /device:TPU:0, one launch (start us, length us, event | category | flops | bytes accessed | tf_op | source)
XLA Modules:
  0.0 41.5 jit_solution(1494133633070265567)
XLA Ops:
  1.3 39.2 %shard_map.130 = (bf16[2,16,4608]{2,1,0:T(8,128)(2,1)S(1)}, f32[16,2,4608]{2,1,0:T(2,128)S(1)}, bf16[1,16,4608]{2,1,0:T(8,128)(2,1)S(1)}) custom-call(s32[4]{0:T(128)} %secs_hbm.1, s32[256]{0:T(256)} %blks_hbm.1, f32[1,1]{1,0:T(1,128)S(6)} %copy.14.loss_hbm, bf16[2,16,4608]{2,1,0:T(8,128)(2,1)} %act_hbm.1, f32[16,2,4608]{2,1,0:T(2,128)} %acc_hbm.1, ...), custom_call_target="tpu_custom_call" | custom-call | tf_op jit(solution)/shard_map/pallas_call | solution.py:473
  40.5 1.0 %shard_map.131 = (bf16[2,16,4608]{2,1,0:T(8,128)(2,1)}, f32[16,2,4608]{2,1,0:T(2,128)}, bf16[1,16,4608]{2,1,0:T(8,128)(2,1)}) custom-call(bf16[2,16,4608]{2,1,0:T(8,128)(2,1)S(1)} %get-tuple-element.6.moved, f32[16,2,4608]{2,1,0:T(2,128)S(1)} %get-tuple-element.7.accout, bf16[1,16,4608]{2,1,0:T(8,128)(2,1)S(1)} %get-tuple-element.8.outbuf), custom_call_target="tpu_custom_call" | custom-call | tf_op jit(solution)/shard_map/pallas_call | solution.py:523

commit v5 on v4

--- a/solution.py
+++ b/solution.py
@@ -70,6 +70,7 @@
     chips = n_dp // 2
     far = chips // 2
     kd = d // CHUNKS
+    half = CHUNKS // 2
     length = n_dp * toks
     hd = wq_hbm.shape[2]
     sec, me = lax.axis_index("section"), lax.axis_index("dp")
@@ -197,8 +198,20 @@
     def width(k):
         return kd + LANES if k == MIXED[-1] else kd
 
+    def order_at(hop):
+        return (MIXED, MIXED) if hop == 1 else AHEAD if hop < far else SORTED
+
+    def await_blocks(columns, sem):
+        view = w.at[pl.ds(0, columns * toks // LANES), pl.ds(0, LANES)]
+        remote(view, view, sem, sem, partner).wait_recv()
+
     def place_of(way, hop, k):
-        return (hop - 1) * 2 * CHUNKS + (way * CHUNKS if hop < far else 0) + k
+        return (hop - 1) * 2 * CHUNKS + (way * CHUNKS + k if hop < far else order_at(hop)[way].index(k))
+
+    def ring_place(way, step, k):
+        if step == hops(way, k):
+            return (2 * far - 3) * CHUNKS + k
+        return (step - 1) * 2 * CHUNKS + (way * CHUNKS if step < far - 1 else 0) + k
 
     def last(k):
         return 1 if k == MIXED[-1] else 0
@@ -230,7 +243,7 @@
 
     def pass_on(j, k):
         block = blocks_of(k, core, j)
-        remote(block, block, fwd_out.at[last(k)], fwd_sem.at[0 if j < near else 1, k], partner).start()
+        remote(block, block, fwd_out.at[last(k)], fwd_sem.at[0 if j < near else 1, k % half], partner).start()
 
     square = jnp.zeros((toks, 1), F32)
     for k in MIXED:
@@ -264,9 +277,7 @@
             ref[index] = terms if fresh else ref[index] + terms
 
         add(qs, span, core, slice(0, 2 * hd))
-        for k in ks:
-            block = blocks_of(k, 1 - core, pl.ds(span.start, count))
-            remote(block, block, fwd_out.at[0], fwd_sem.at[part_of, k], partner).wait_recv()
+        await_blocks(count * sum(width(k) for k in ks), fwd_sem.at[part_of, ks[0] % half])
         add(kvs, (slice(None), span), slice(None), slice(2 * hd, 4 * hd))
 
     three = w.at[:, pl.ds(0, 3 * hd)]
@@ -286,13 +297,15 @@
             for t in range(2):
                 turn[t, c, j] = rot[t, place, (c + (j + 1) // 2) % 2]
 
-    half = CHUNKS // 2
     for hop in range(1, far + 1):
-        order = (MIXED, MIXED) if hop == 1 else AHEAD if hop < far else SORTED
+        order = order_at(hop)
         for i in range(CHUNKS if hop < far else half):
+            if hop == far:
+                await_blocks(sum(width(order[way][i]) for way in range(2)), ag_sem.at[place_of(0, hop, order[0][i])])
             for way in range(2):
                 k = order[way][i]
-                gather_copy(way, hop, k).wait_recv()
+                if hop < far:
+                    gather_copy(way, hop, k).wait_recv()
                 forward(way, hop, k)
                 pass_on(slot(way, hop), k)
             if hop == 1:
@@ -306,7 +319,7 @@
                     send_block(other)
             if hop == 2:
                 share(wo.at[wo_rows, pl.ds(i * kd, kd)], 2)
-            if hop == far - 1 and i == CHUNKS - 1:
+            if hop == far - 1 and i == CHUNKS - 2:
                 send_blocks([(way, far - h) for h in range(1, far - 1) for way in range(2)])
             if hop == far - 1 and i == 1:
                 weights.wait_recv()
@@ -347,7 +360,7 @@
         if hops(way, k) - step + 1 > cross:
             goal = {"dp": jnp.where(from_middle[1 - way], mate["dp"], goal["dp"])}
         return remote(ring_out.at[k, way * far + step - 1], ring_in.at[k, way * far + step - 1],
-                      ring_done.at[0], ring_sem.at[place_of(way, step, k)], goal)
+                      ring_done.at[0], ring_sem.at[ring_place(way, step, k)], goal)
 
     def crossing(way, step, k):
         return hops(way, k) - step + 1 > cross
@@ -418,14 +431,15 @@
 
     lax.fori_loop(0, blk, unpack, 0)
 
-    pieces = []
-    for k in range(CHUNKS):
+    loads["post"].wait()
+    pieces, square = [None] * CHUNKS, jnp.zeros((toks, 1), F32)
+    for k in MIXED:
+        await_blocks(2 * kd, ring_sem.at[ring_place(0, hops(0, k), k)])
         total = part[k, 0]
         for way in range(2):
-            total = total + take(way, hops(way, k), k)
-        pieces.append(total)
-    loads["post"].wait()
-    square = sum(jnp.sum(t * t, axis=-1, keepdims=True) for t in pieces)
+            total = total + ring_in[k, way * far + hops(way, k) - 1].astype(F32)
+        pieces[k] = total
+        square = square + jnp.sum(total * total, axis=-1, keepdims=True)
     scale = lax.rsqrt(square / d + 1e-06)
     for k in range(CHUNKS):
         cols = slice(k * kd, (k + 1) * kd)
@@ -509,11 +523,11 @@
                 dma((4,)),
                 dma((2,)),
                 dma((2,)),
-                dma(((2 * far - 1) * CHUNKS,)),
+                dma((2 * (far - 1) * CHUNKS + CHUNKS // 2,)),
                 dma((2,)),
-                dma((2, CHUNKS)),
+                dma((2, CHUNKS // 2)),
                 dma((1,)),
-                dma(((2 * far - 1) * CHUNKS,)),
+                dma((2 * (far - 1) * CHUNKS,)),
             ],
             compiler_params=pltpu.CompilerParams(
                 collective_id=0, has_side_effects=True, vmem_limit_bytes=VMEM_BYTES - 2**16 - out_bytes

time: 41.7 us -> 41.5 us (level)
  no operation moved by 1% of the time
where the time goes in v5:
time: 41.5 us; the launch traced here: 41.4 us
  Pallas kernels  40.1 us (97%)
  between operations  1.29 us (3%)
    pallas_call x1, Pallas kernels, on_device(): pl.pallas_call(functools.partial(kernel, (n_sec, n_dp)), out_shape=(pltpu...  39.1 us
    pallas_call x1, Pallas kernels, on_device(): pl.pallas_call(write_out, out_shape=(jax.ShapeDtypeStruct(activations.sha...  0.98 us

profile of v5, /device:TPU:0, one launch (start us, length us, event | category | flops | bytes accessed | tf_op | source)
XLA Modules:
  0.0 41.4 jit_solution(7864763948150944694)
XLA Ops:
  1.3 39.1 %shard_map.130 = (bf16[2,16,4608]{2,1,0:T(8,128)(2,1)S(1)}, f32[16,2,4608]{2,1,0:T(2,128)S(1)}, bf16[1,16,4608]{2,1,0:T(8,128)(2,1)S(1)}) custom-call(s32[4]{0:T(128)} %secs_hbm.1, s32[256]{0:T(256)} %blks_hbm.1, f32[1,1]{1,0:T(1,128)S(6)} %copy.14.loss_hbm, bf16[2,16,4608]{2,1,0:T(8,128)(2,1)} %act_hbm.1, f32[16,2,4608]{2,1,0:T(2,128)} %acc_hbm.1, ...), custom_call_target="tpu_custom_call" | custom-call | tf_op jit(solution)/shard_map/pallas_call | solution.py:487
  40.4 1.0 %shard_map.131 = (bf16[2,16,4608]{2,1,0:T(8,128)(2,1)}, f32[16,2,4608]{2,1,0:T(2,128)}, bf16[1,16,4608]{2,1,0:T(8,128)(2,1)}) custom-call(bf16[2,16,4608]{2,1,0:T(8,128)(2,1)S(1)} %get-tuple-element.6.moved, f32[16,2,4608]{2,1,0:T(2,128)S(1)} %get-tuple-element.7.accout, bf16[1,16,4608]{2,1,0:T(8,128)(2,1)S(1)} %get-tuple-element.8.outbuf), custom_call_target="tpu_custom_call" | custom-call | tf_op jit(solution)/shard_map/pallas_call | solution.py:537
